TPU v7x, 32 devices: a whole 2x2x4 slice. The times are simulated.
32 devices in a mesh: grp: 4 (over z), seq: 8 (over y, x, core).
Axes of the slice: x: 2, y: 2, z: 4, core: 2. Of those that a mesh axis runs over, the one named last changes fastest.
Arguments:
- hidden_in: bfloat16 [24, 4096], P(None, ('grp', 'seq')), may hold values from -6 to 6
- norm_gain: float32 [4096], replicated, may hold values from 0.5 to 1.5
- w_ssm_in: bfloat16 [4096, 8192], P(None, ('grp', 'seq')), may hold values from -0.09375 to 0.09375
- w_ssm_gate: bfloat16 [4096, 8192], P(None, ('grp', 'seq')), may hold values from -0.09375 to 0.09375
- conv_weight: float32 [4, 8192], P(None, ('grp', 'seq')), may hold values from -3 to 3
- conv_bias: float32 [8192], P(('grp', 'seq')), may hold values from -0.5 to 0.5
- conv_state: bfloat16 [24, 3, 8192], P(None, None, ('grp', 'seq')), may hold values from -6 to 6
- w_state_proj: bfloat16 [8192, 288], P(('grp', 'seq')), may hold values from -0.0625 to 0.0625
- w_step: bfloat16 [256, 8192], P(None, ('grp', 'seq')), may hold values from -0.375 to 0.375
- step_bias: float32 [8192], P(('grp', 'seq')), may hold values from -4 to -1
- log_decay: float32 [16, 8192], P(None, ('grp', 'seq')), may hold values from 0 to 2.7
- skip_gain: float32 [8192], P(('grp', 'seq')), may hold values from 0.5 to 1.5
- ssm_state: float32 [24, 16, 8192], P(None, None, ('grp', 'seq')), may hold values from -6 to 6
- w_ssm_out: bfloat16 [8192, 4096], P(('grp', 'seq')), may hold values from -0.125 to 0.125
- w_query: bfloat16 [4096, 2048], P(None, 'grp'), may hold values from -6 to 6
- key_projection: bfloat16 [4096, 1024], P(None, 'grp'), may hold values from -0.09375 to 0.09375
- value_projection: bfloat16 [4096, 1024], P(None, 'grp'), may hold values from -0.09375 to 0.09375
- w_attn_out: bfloat16 [2048, 4096], P('grp', 'seq'), may hold values from -0.125 to 0.125
- w_mlp_gate: bfloat16 [4096, 14336], P(None, ('grp', 'seq')), may hold values from -0.09375 to 0.09375
- w_mlp_up: bfloat16 [4096, 14336], P(None, ('grp', 'seq')), may hold values from -0.09375 to 0.09375
- w_mlp_down: bfloat16 [14336, 4096], P(('grp', 'seq')), may hold values from -0.09375 to 0.09375
- cached_inputs: bfloat16 [24, 512, 4096], P('seq'), may hold values from -6 to 6
- window_lengths: int32 [24], replicated, may hold values from 1 to 512, as said below
Outputs:
- hidden_out: bfloat16 [24, 4096], P(None, ('grp', 'seq'))
- state_out: float32 [24, 16, 8192], P(None, None, ('grp', 'seq'))
Inputs may be any that keep to these rules, and one draw needn't show every extreme that they name: `window_lengths`: every sequence has at least one valid cached position, and some sequence fills the whole window of 512.
All inputs are finite; a program needn't handle non-finite values.
Results may differ from a plain program's by a relative error of at most 0.012.
The roundings to bfloat16 on the way count: a program that leaves them out, or rounds other values in their place, can miss the bound.
Values may be sent and summed in bfloat16 or wider, within the bound.
No kernel may reach another device: no remote copies, remote signals or barrier semaphores. Data moves between devices by JAX's collectives and lax.ppermute only.
A program may use at most 128 MiB of HBM per device.

v0:
```python
import jax
import jax.numpy as jnp
from jax import lax
from jax.sharding import PartitionSpec as P

HEAD_SIZE = 128
epsilon = 1e-05
rope_base = 10000.0


def apply_rotary(head_values, positions):
    half_dim = head_values.shape[-1] // 2
    frequency = rope_base ** (
        -(jnp.arange(half_dim, dtype=jnp.float32) * 2.0) / head_values.shape[-1]
    )
    angles = positions[..., None, None] * frequency
    cosine = jnp.cos(angles)
    sine_part = jnp.sin(angles)
    front_half = head_values[..., :half_dim]
    back_half = head_values[..., half_dim:]
    return jnp.concatenate(
        [front_half * cosine - back_half * sine_part, back_half * cosine + front_half * sine_part],
        axis=-1,
    )


def per_device(
    hidden_in,
    norm_gain,
    w_ssm_in,
    w_ssm_gate,
    conv_weight,
    conv_bias,
    conv_state,
    w_state_proj,
    w_step,
    step_bias,
    log_decay,
    skip_gain,
    ssm_state,
    w_ssm_out,
    w_query,
    key_projection,
    value_projection,
    w_attn_out,
    w_mlp_gate,
    w_mlp_up,
    w_mlp_down,
    cached_inputs,
    window_lengths,
):
    batch_rows = hidden_in.shape[0]
    model_width = norm_gain.shape[0]
    hidden_f = hidden_in.astype(jnp.float32)
    raw_full = lax.all_gather(hidden_in, ("grp", "seq"), axis=1, tiled=True).astype(jnp.float32)
    row_scale = lax.rsqrt(jnp.mean(raw_full * raw_full, axis=1, keepdims=True) + epsilon)
    normed_input = (raw_full * row_scale * norm_gain).astype(jnp.bfloat16)
    ssm_input = jnp.dot(normed_input, w_ssm_in, preferred_element_type=jnp.float32).astype(
        jnp.bfloat16
    )
    gate_input = jnp.dot(normed_input, w_ssm_gate, preferred_element_type=jnp.float32)
    past_inputs = conv_state.astype(jnp.float32)
    conv_sum = (
        conv_bias
        + jnp.sum(past_inputs * conv_weight[:-1][None], axis=1)
        + conv_weight[-1] * lax.optimization_barrier(ssm_input).astype(jnp.float32)
    )
    conv_out = jax.nn.silu(conv_sum)
    rank_size = w_step.shape[0]
    state_size = log_decay.shape[0]
    low_rank = lax.psum(
        jnp.dot(conv_out.astype(jnp.bfloat16), w_state_proj, preferred_element_type=jnp.float32),
        ("grp", "seq"),
    )
    step_low = low_rank[:, :rank_size].astype(jnp.bfloat16)
    input_map = low_rank[:, rank_size : rank_size + state_size]
    output_map = low_rank[:, rank_size + state_size :]
    step_size = jax.nn.softplus(
        jnp.dot(step_low, w_step, preferred_element_type=jnp.float32) + step_bias
    )
    decay_rate = jnp.exp(log_decay)
    state_out = (
        jnp.exp(-step_size[:, None, :] * decay_rate[None]) * ssm_state
        + step_size[:, None, :] * input_map[:, :, None] * conv_out[:, None, :]
    )
    ssm_mixed = jnp.sum(state_out * output_map[:, :, None], axis=1) + skip_gain * conv_out
    ssm_gated = (ssm_mixed * jax.nn.silu(gate_input)).astype(jnp.bfloat16)
    ssm_term = jnp.dot(ssm_gated, w_ssm_out, preferred_element_type=jnp.float32)
    ssm_summed = lax.psum_scatter(ssm_term, ("grp", "seq"), scatter_dimension=1, tiled=True)
    gate_act = jnp.dot(normed_input, w_mlp_gate, preferred_element_type=jnp.float32)
    up_act = jnp.dot(normed_input, w_mlp_up, preferred_element_type=jnp.float32)
    mlp_hidden = (jax.nn.silu(gate_act) * up_act).astype(jnp.bfloat16)
    mlp_term = jnp.dot(mlp_hidden, w_mlp_down, preferred_element_type=jnp.float32)
    own_seqs = cached_inputs.shape[0]
    window_size = cached_inputs.shape[1]
    seq_start = lax.axis_index("seq") * own_seqs
    normed_own = lax.dynamic_slice_in_dim(normed_input, seq_start, own_seqs, 0)
    lengths_own = lax.dynamic_slice_in_dim(window_lengths, seq_start, own_seqs, 0)
    heads_here = w_query.shape[1] // HEAD_SIZE
    kv_here = key_projection.shape[1] // HEAD_SIZE
    heads_per_group = heads_here // kv_here
    attention_scale = HEAD_SIZE ** (-0.5)
    fresh_position = lengths_own.astype(jnp.float32)
    query = apply_rotary(
        jnp.dot(normed_own, w_query, preferred_element_type=jnp.float32).reshape(
            own_seqs, heads_here, HEAD_SIZE
        ),
        fresh_position,
    ).astype(jnp.bfloat16)
    fresh_key = apply_rotary(
        jnp.dot(normed_own, key_projection, preferred_element_type=jnp.float32).reshape(
            own_seqs, kv_here, HEAD_SIZE
        ),
        fresh_position,
    ).astype(jnp.bfloat16)
    fresh_value = (
        jnp.dot(normed_own, value_projection, preferred_element_type=jnp.float32)
        .astype(jnp.bfloat16)
        .reshape(own_seqs, kv_here, HEAD_SIZE)
    )
    flat_inputs = cached_inputs.reshape(own_seqs * window_size, model_width)
    slot_ids = jnp.arange(window_size, dtype=jnp.int32)
    positions = jnp.broadcast_to(slot_ids[None, :], (own_seqs, window_size)).astype(jnp.float32)
    window_key_rows = jnp.dot(
        flat_inputs, key_projection, preferred_element_type=jnp.float32
    ).reshape(own_seqs, window_size, kv_here, HEAD_SIZE)
    window_key_rows = apply_rotary(window_key_rows, positions).astype(jnp.bfloat16)
    window_value_rows = (
        jnp.dot(flat_inputs, value_projection, preferred_element_type=jnp.float32)
        .astype(jnp.bfloat16)
        .reshape(own_seqs, window_size, kv_here, HEAD_SIZE)
    )
    grouped_query = query.astype(jnp.float32).reshape(own_seqs, kv_here, heads_per_group, HEAD_SIZE)
    scores = (
        jnp.einsum("bkgd,bpkd->bkgp", grouped_query, window_key_rows.astype(jnp.float32))
        * attention_scale
    )
    fresh_score = (
        jnp.einsum("ynow,ynw->yno", grouped_query, fresh_key.astype(jnp.float32)) * attention_scale
    )
    is_valid = (slot_ids[None, :] < lengths_own[:, None])[:, None, None, :]
    scores = jnp.where(is_valid, scores, -1e30)
    joint_max = jnp.maximum(jnp.max(scores, axis=-1), fresh_score)
    weights = jnp.where(is_valid, jnp.exp(scores - joint_max[..., None]), 0.0)
    weight_new = jnp.exp(fresh_score - joint_max)
    joint_total = jnp.sum(weights, axis=-1) + weight_new
    joint_sum = (
        jnp.einsum("bkgp,bpkd->bkgd", weights, window_value_rows.astype(jnp.float32))
        + weight_new[..., None] * fresh_value.astype(jnp.float32)[:, :, None, :]
    )
    attended_own = (
        (joint_sum / joint_total[..., None])
        .reshape(own_seqs, heads_here * HEAD_SIZE)
        .astype(jnp.bfloat16)
    )
    attended = lax.all_gather(attended_own, "seq", axis=0, tiled=True)
    attn_cols = jnp.dot(attended, w_attn_out, preferred_element_type=jnp.float32)
    col_start = lax.axis_index("seq") * w_attn_out.shape[1]
    attn_term = lax.dynamic_update_slice(
        jnp.zeros((batch_rows, model_width), jnp.float32), attn_cols, (jnp.int32(0), col_start)
    )
    other_terms = mlp_term + attn_term
    summed = ssm_summed + lax.psum_scatter(
        other_terms, ("grp", "seq"), scatter_dimension=1, tiled=True
    )
    hidden_out = (hidden_f + summed).astype(jnp.bfloat16)
    return (hidden_out, state_out)


def solution(mesh):
    placed = (
        P(None, ("grp", "seq")),
        P(),
        P(None, ("grp", "seq")),
        P(None, ("grp", "seq")),
        P(None, ("grp", "seq")),
        P(("grp", "seq")),
        P(None, None, ("grp", "seq")),
        P(("grp", "seq"), None),
        P(None, ("grp", "seq")),
        P(("grp", "seq")),
        P(None, ("grp", "seq")),
        P(("grp", "seq")),
        P(None, None, ("grp", "seq")),
        P(("grp", "seq"), None),
        P(None, "grp"),
        P(None, "grp"),
        P(None, "grp"),
        P("grp", "seq"),
        P(None, ("grp", "seq")),
        P(None, ("grp", "seq")),
        P(("grp", "seq"), None),
        P("seq", None, None),
        P(),
    )
    return jax.shard_map(
        per_device,
        mesh=mesh,
        in_specs=placed,
        out_specs=(P(None, ("grp", "seq")), P(None, None, ("grp", "seq"))),
        check_vma=False,
    )
```

profile of v0, /device:TPU:0, one launch (start us, length us, event | category | flops | bytes accessed | tf_op | source)
XLA Modules:
  0.0 289.1 jit_solution(317169863830582743)
XLA Ops:
  7.3 44.2 %all_gather.6 = bf16[24,4096]{1,0:T(8,128)(2,1)S(1)} all-gather(bf16[24,128]{1,0:T(8,128)(2,1)} %param.23), channel_id=1, replica_groups=mesh['grp'=4,'seq'=8] {'grp','seq'}, dimensions={1}, use_global_device_ids=true | all-gather | bytes 202752 | tf_op jit(solution)/shard_map/all_gather | solution.py:55
  51.4 0.2 fusion.13
  51.6 0.8 fusion.15
  52.5 2.8 fusion.25
  55.3 0.1 fusion.42
  55.5 0.1 multiply_cosine_fusion.1
  55.6 0.5 multiply_cosine_fusion
  56.1 2.0 fusion.23
  58.1 4.1 %copy.38 = bf16[256,4096]{1,0:T(8,128)(2,1)} copy(bf16[256,4096]{0,1:T(8,128)(2,1)} %bitcast.38) | data formatting | bytes 4194304 | tf_op jit(solution)/shard_map/dot_general | solution.py:124
  62.2 0.1 subtract_convert_fusion.1
  62.3 7.1 %fusion = f32[3,512,2,128]{1,3,2,0:T(8,128)S(1)} fusion(bf16[2,128,4096,1]{2,1,0,3:T(8,128)(2,1)} %bitcast.39, bf16[3,512,4096]{2,1,0:T(8,128)(2,1)} %param.44), kind=kOutput, calls=%fused_computation | convolution fusion | flops 3221225472 | bytes 16252928 | tf_op jit(solution)/shard_map/dot_general | solution.py:124
  69.5 0.1 maximum_bitcast_fusion
  69.6 0.3 subtract_convert_fusion
  69.9 0.2 fusion.32
  70.1 0.3 fusion.44
  70.5 0.2 fusion.31
  70.7 0.4 fusion.8
  71.1 7.4 %convolution_convert_fusion = bf16[1536,256]{1,0:T(8,128)(2,1)} fusion(bf16[1536,4096]{1,0:T(8,128)(2,1)} %bitcast.48, bf16[4096,256]{1,0:T(8,128)(2,1)S(1)} %copy-done), kind=kOutput, calls=%fused_computation.3 | convolution fusion | flops 3221618688 | bytes 15466496 | tf_op jit(solution)/shard_map/dot_general | solution.py:129
  78.4 2.0 reshape.155
  80.5 0.3 fusion.7
  80.8 7.0 %all-gather = bf16[8,3,512]{2,1,0:T(4,128)(2,1)S(1)} all-gather(bf16[1,3,512]{2,1,0:T(4,128)(2,1)S(1)} %reshape.157), channel_id=1, replica_groups=mesh['grp'=4,'seq'=8] {'seq'}, dimensions={0}, use_global_device_ids=true | all-gather | bytes 27648 | tf_op jit(solution)/shard_map/all_gather | solution.py:156
  87.8 3.1 %fusion.48 = f32[24,448]{1,0:T(8,128)S(1)} fusion(bf16[24,4096]{1,0:T(8,128)(2,1)S(1)} %fusion.15, bf16[4096,448]{0,1:T(8,128)(2,1)} %param.41), kind=kOutput, calls=%fused_computation.85 | convolution fusion | flops 88080384 | bytes 3909632 | tf_op jit(solution)/shard_map/dot_general | solution.py:90
  91.0 2.1 convolution_convert_fusion.1
  93.2 0.2 fusion.28
  93.4 38.3 %psum.7 = f32[24,288]{1,0:T(8,128)S(1)} all-reduce(f32[24,288]{1,0:T(8,128)S(1)} %fusion.28), channel_id=1, replica_groups=mesh['grp'=4,'seq'=8] {'grp','seq'}, use_global_device_ids=true, to_apply=%region_2.3 | all-reduce | flops 6912 | bytes 55296 | tf_op jit(solution)/shard_map/psum | solution.py:71
  131.8 0.2 fusion.45
  132.0 5.1 %fusion.4 = f32[24,4096]{1,0:T(8,128)S(1)} fusion(bf16[448,4096]{1,0:T(8,128)(2,1)} %param.43, bf16[24,4096]{1,0:T(8,128)(2,1)S(1)} %fusion.15, bf16[4096,448]{0,1:T(8,128)(2,1)} %param.42, f32[24,448]{1,0:T(8,128)S(1)} %fusion.48), kind=kOutput, calls=%fused_computation.8 | convolution fusion | flops 176225280 | bytes 7972864 | tf_op jit(solution)/shard_map/dot_general | solution.py:93
  137.1 0.2 fusion.2
  137.3 1.9 multiply_reduce_fusion
  139.3 4.3 %convolution_add_fusion = f32[24,4096]{1,0:T(8,128)} fusion(f32[24,4096]{1,0:T(8,128)S(1)} %fusion.2, bf16[256,4096]{1,0:T(8,128)(2,1)} %param.36, f32[24,256]{1,0:T(8,128)S(1)} %get-tuple-element.2, f32[24,256]{1,0:T(8,128)S(1)} %divide_multiply_fusion, f32[256]{0:T(256)S(1)} %copy-done.10, bf16[24,4096]{1,0:T(8,128)(2,1)S(1)} %fusion.15, ...), kind=kOutput, calls=%fused_computation.2 | convolution fusion | flops 100810752 | bytes 5227520 | tf_op jit(solution)/shard_map/dot_general | solution.py:88
  143.6 137.4 %reduce-scatter.2.cloned.1.call-done = f32[24,128]{1,0:T(8,128)} async-done(((f32[24,4096]{1,0:T(8,128)}), f32[24,128]{1,0:T(8,128)}) %reduce-scatter.2.cloned.1.call-update) | async-done | bytes 12304 | tf_op jit(solution)/shard_map/reduce_scatter | solution.py:89
  280.9 1.3 add_convert_fusion.1
  (43 shorter events, 0.6 us)
Async XLA Ops:
  7.2 63.5 %copy-start = (bf16[4096,256]{1,0:T(8,128)(2,1)S(1)}, bf16[4096,256]{1,0:T(8,128)(2,1)}, u32[]{:S(2)}) copy-start(bf16[4096,256]{1,0:T(8,128)(2,1)} %param.39) | copy-start | bytes 6291460
  7.2 273.8 %reduce-scatter.2.cloned.1.call-start = ((), (), s32[]{:S(2)}) async-start(), calls=%async_computation.1 | async-start | bytes 405504 | tf_op jit(solution)/shard_map/reduce_scatter | solution.py:89
  52.4 2.9 copy-start.11
  90.9 2.2 copy-start.7
  90.9 2.2 copy-start.4
  91.0 2.2 copy-start.8
  91.0 2.2 copy-start.2
  91.0 40.8 %copy-start.6 = (f32[16,256]{1,0:T(8,128)S(1)}, f32[16,256]{1,0:T(8,128)}, u32[]{:S(2)}) copy-start(f32[16,256]{1,0:T(8,128)} %param.33) | copy-start | bytes 49156
  91.0 40.8 %copy-start.3 = (bf16[256,256]{1,0:T(8,128)(2,1)S(1)}, bf16[256,256]{1,0:T(8,128)(2,1)}, u32[]{:S(2)}) copy-start(bf16[256,256]{1,0:T(8,128)(2,1)} %param.31) | copy-start | bytes 393220
  91.0 40.8 %copy-start.9 = (f32[256]{0:T(256)S(1)}, f32[256]{0:T(256)}, u32[]{:S(2)}) copy-start(f32[256]{0:T(256)} %param.32) | copy-start | bytes 3076
  132.0 5.1 %copy-start.1 = (bf16[512,512]{1,0:T(8,128)(2,1)S(1)}, bf16[512,512]{1,0:T(8,128)(2,1)}, u32[]{:S(2)}) copy-start(bf16[512,512]{1,0:T(8,128)(2,1)} %param.40) | copy-start | bytes 1572868
  132.0 7.2 %copy-start.10 = (f32[256]{0:T(256)S(1)}, f32[256]{0:T(256)}, u32[]{:S(2)}) copy-start(f32[256]{0:T(256)} %param.34) | copy-start | bytes 3076
  139.3 141.7 %copy-start.5 = (bf16[24,128]{1,0:T(8,128)(2,1)S(1)}, bf16[24,128]{1,0:T(8,128)(2,1)}, u32[]{:S(2)}) copy-start(bf16[24,128]{1,0:T(8,128)(2,1)} %param.23) | copy-start | bytes 18436
Sparse Core Ops, SparseCore 0:
  143.7 137.2 reduce-scatter.1
where the time goes:
time: 290 us; the launch traced here: 289 us
  waiting for transfers between devices  137 us (47%)
  blocking collectives  89.5 us (31%)
  matrix products  35.6 us (12%)
  between operations  14.3 us (5%)
  local copies, waits for them, and re-layouts  6.37 us (2%)
  other arithmetic  5.87 us (2%)
    reduce_scatter x1, waiting for transfers between devices, per_device(): lax.psum_scatter(ssm_term, ('grp', 'seq'), scatter_dimension=1, tiled=True)  137 us
    all_gather x1, blocking collectives, per_device(): lax.all_gather(hidden_in, ('grp', 'seq'), axis=1, tiled=True)  44.2 us
    psum x1, blocking collectives, per_device(): lax.psum(jnp.dot(conv_out.astype(jnp.bfloat16), w_state_proj, preferred_e...  38.3 us
    dot_general x1, matrix products, per_device(): jnp.dot(flat_inputs, value_projection, preferred_element_type=jnp.float32)  7.38 us
    dot_general x1, matrix products, per_device(): jnp.dot(flat_inputs, key_projection, preferred_element_type=jnp.float32)  7.13 us
    all_gather x1, blocking collectives, per_device(): attended = lax.all_gather(attended_own, 'seq', axis=0, tiled=True)  7.02 us
  transfers between devices with their start and end apart: 1, of which 1 were waited for; matrix products, arithmetic and copies ran while one was open for 0% of the time, Pallas kernels for 0%

commit v1 on v0

--- a/solution.py
+++ b/solution.py
@@ -69,8 +69,13 @@
     rank_size = w_step.shape[0]
     state_size = log_decay.shape[0]
     low_rank = lax.psum(
-        jnp.dot(conv_out.astype(jnp.bfloat16), w_state_proj, preferred_element_type=jnp.float32),
-        ("grp", "seq"),
+        lax.psum(
+            jnp.dot(
+                conv_out.astype(jnp.bfloat16), w_state_proj, preferred_element_type=jnp.float32
+            ),
+            "seq",
+        ),
+        "grp",
     )
     step_low = low_rank[:, :rank_size].astype(jnp.bfloat16)
     input_map = low_rank[:, rank_size : rank_size + state_size]

time: 290 us -> 290 us (level)
    psum x0 -> x1, blocking collectives: none -> 16.2 us  [per_device(): lax.psum(lax.psum(jnp.dot(conv_out.astype(jnp.bfloat16), w_state_proj, pr...]
    psum x1, blocking collectives: 38.3 us -> 24.8 us  [per_device(): lax.psum(jnp.dot(conv_out.astype(jnp.bfloat16), w_state_proj, preferred_e...]
where the time goes in v1:
time: 290 us; the launch traced here: 289 us
  waiting for transfers between devices  135 us (47%)
  blocking collectives  92.3 us (32%)
  matrix products  35.6 us (12%)
  between operations  14.3 us (5%)
  local copies, waits for them, and re-layouts  6.4 us (2%)
  other arithmetic  5.87 us (2%)
    reduce_scatter x1, waiting for transfers between devices, per_device(): lax.psum_scatter(ssm_term, ('grp', 'seq'), scatter_dimension=1, tiled=True)  135 us
    all_gather x1, blocking collectives, per_device(): lax.all_gather(hidden_in, ('grp', 'seq'), axis=1, tiled=True)  44.2 us
    psum x1, blocking collectives, per_device(): lax.psum(jnp.dot(conv_out.astype(jnp.bfloat16), w_state_proj, preferred_e...  24.8 us
    psum x1, blocking collectives, per_device(): lax.psum(lax.psum(jnp.dot(conv_out.astype(jnp.bfloat16), w_state_proj, pr...  16.2 us
    dot_general x1, matrix products, per_device(): jnp.dot(flat_inputs, value_projection, preferred_element_type=jnp.float32)  7.38 us
    dot_general x1, matrix products, per_device(): jnp.dot(flat_inputs, key_projection, preferred_element_type=jnp.float32)  7.14 us
    all_gather x1, blocking collectives, per_device(): attended = lax.all_gather(attended_own, 'seq', axis=0, tiled=True)  7.02 us
  transfers between devices with their start and end apart: 1, of which 1 were waited for; matrix products, arithmetic and copies ran while one was open for 0% of the time, Pallas kernels for 0%

profile of v1, /device:TPU:0, one launch (start us, length us, event | category | flops | bytes accessed | tf_op | source)
XLA Modules:
  0.0 289.2 jit_solution(6163291654230625179)
XLA Ops:
  7.3 44.2 %all_gather.6 = bf16[24,4096]{1,0:T(8,128)(2,1)S(1)} all-gather(bf16[24,128]{1,0:T(8,128)(2,1)} %param.23), channel_id=1, replica_groups=mesh['grp'=4,'seq'=8] {'grp','seq'}, dimensions={1}, use_global_device_ids=true | all-gather | bytes 202752 | tf_op jit(solution)/shard_map/all_gather | solution.py:55
  51.4 0.2 fusion.13
  51.6 0.8 fusion.15
  52.5 2.8 fusion.25
  55.3 0.1 fusion.42
  55.5 0.1 multiply_cosine_fusion.1
  55.6 0.5 multiply_cosine_fusion
  56.1 2.0 fusion.23
  58.1 4.1 %copy.38 = bf16[256,4096]{1,0:T(8,128)(2,1)} copy(bf16[256,4096]{0,1:T(8,128)(2,1)} %bitcast.38) | data formatting | bytes 4194304 | tf_op jit(solution)/shard_map/dot_general | solution.py:129
  62.4 7.1 %fusion = f32[3,512,2,128]{1,3,2,0:T(8,128)S(1)} fusion(bf16[2,128,4096,1]{2,1,0,3:T(8,128)(2,1)} %bitcast.39, bf16[3,512,4096]{2,1,0:T(8,128)(2,1)} %param.44), kind=kOutput, calls=%fused_computation | convolution fusion | flops 3221225472 | bytes 16252928 | tf_op jit(solution)/shard_map/dot_general | solution.py:129
  69.5 0.1 maximum_bitcast_fusion
  69.6 0.3 subtract_convert_fusion
  69.9 0.2 fusion.32
  70.1 0.3 fusion.44
  70.5 0.2 fusion.31
  70.7 0.4 fusion.8
  71.1 7.4 %convolution_convert_fusion = bf16[1536,256]{1,0:T(8,128)(2,1)} fusion(bf16[1536,4096]{1,0:T(8,128)(2,1)} %bitcast.48, bf16[4096,256]{1,0:T(8,128)(2,1)S(1)} %copy-done), kind=kOutput, calls=%fused_computation.3 | convolution fusion | flops 3221618688 | bytes 15466496 | tf_op jit(solution)/shard_map/dot_general | solution.py:134
  78.5 2.0 reshape.155
  80.5 0.3 fusion.7
  80.8 7.0 %all-gather = bf16[8,3,512]{2,1,0:T(4,128)(2,1)S(1)} all-gather(bf16[1,3,512]{2,1,0:T(4,128)(2,1)S(1)} %reshape.157), channel_id=1, replica_groups=mesh['grp'=4,'seq'=8] {'seq'}, dimensions={0}, use_global_device_ids=true | all-gather | bytes 27648 | tf_op jit(solution)/shard_map/all_gather | solution.py:161
  87.9 3.1 %fusion.48 = f32[24,448]{1,0:T(8,128)S(1)} fusion(bf16[24,4096]{1,0:T(8,128)(2,1)S(1)} %fusion.15, bf16[4096,448]{0,1:T(8,128)(2,1)} %param.41), kind=kOutput, calls=%fused_computation.85 | convolution fusion | flops 88080384 | bytes 3909632 | tf_op jit(solution)/shard_map/dot_general | solution.py:95
  91.1 2.1 convolution_convert_fusion.1
  93.2 0.2 fusion.28
  93.4 24.8 %psum.14 = f32[24,288]{1,0:T(8,128)S(1)} all-reduce(f32[24,288]{1,0:T(8,128)S(1)} %fusion.28), channel_id=1, replica_groups=mesh['grp'=4,'seq'=8] {'seq'}, use_global_device_ids=true, to_apply=%region_2.3 | all-reduce | flops 6912 | bytes 55296 | tf_op jit(solution)/shard_map/psum | solution.py:72
  118.2 16.2 %psum.15 = f32[24,288]{1,0:T(8,128)S(1)} all-reduce(f32[24,288]{1,0:T(8,128)S(1)} %psum.14), channel_id=1, replica_groups=mesh['grp'=4,'seq'=8] {'grp'}, use_global_device_ids=true, to_apply=%region_3.4 | all-reduce | flops 6912 | bytes 55296 | tf_op jit(solution)/shard_map/psum | solution.py:71
  134.6 0.2 fusion.45
  134.8 5.1 %fusion.4 = f32[24,4096]{1,0:T(8,128)S(1)} fusion(bf16[448,4096]{1,0:T(8,128)(2,1)} %param.43, bf16[24,4096]{1,0:T(8,128)(2,1)S(1)} %fusion.15, bf16[4096,448]{0,1:T(8,128)(2,1)} %param.42, f32[24,448]{1,0:T(8,128)S(1)} %fusion.48), kind=kOutput, calls=%fused_computation.8 | convolution fusion | flops 176225280 | bytes 7972864 | tf_op jit(solution)/shard_map/dot_general | solution.py:98
  139.9 0.2 fusion.2
  140.1 1.9 multiply_reduce_fusion
  142.0 4.3 %convolution_add_fusion = f32[24,4096]{1,0:T(8,128)} fusion(f32[24,4096]{1,0:T(8,128)S(1)} %fusion.2, bf16[256,4096]{1,0:T(8,128)(2,1)} %param.36, f32[24,256]{1,0:T(8,128)S(1)} %get-tuple-element.2, f32[24,256]{1,0:T(8,128)S(1)} %divide_multiply_fusion, f32[256]{0:T(256)S(1)} %copy-done.10, bf16[24,4096]{1,0:T(8,128)(2,1)S(1)} %fusion.15, ...), kind=kOutput, calls=%fused_computation.2 | convolution fusion | flops 100810752 | bytes 5227520 | tf_op jit(solution)/shard_map/dot_general | solution.py:93
  146.4 134.7 %reduce-scatter.2.cloned.1.call-done = f32[24,128]{1,0:T(8,128)} async-done(((f32[24,4096]{1,0:T(8,128)}), f32[24,128]{1,0:T(8,128)}) %reduce-scatter.2.cloned.1.call-update) | async-done | bytes 12304 | tf_op jit(solution)/shard_map/reduce_scatter | solution.py:94
  281.1 1.3 add_convert_fusion.1
  (44 shorter events, 0.6 us)
Async XLA Ops:
  7.2 63.5 %copy-start = (bf16[4096,256]{1,0:T(8,128)(2,1)S(1)}, bf16[4096,256]{1,0:T(8,128)(2,1)}, u32[]{:S(2)}) copy-start(bf16[4096,256]{1,0:T(8,128)(2,1)} %param.39) | copy-start | bytes 6291460
  7.2 273.9 %reduce-scatter.2.cloned.1.call-start = ((), (), s32[]{:S(2)}) async-start(), calls=%async_computation.1 | async-start | bytes 405504 | tf_op jit(solution)/shard_map/reduce_scatter | solution.py:94
  52.4 2.9 copy-start.11
  91.0 2.2 copy-start.7
  91.0 2.2 copy-start.4
  91.0 2.2 copy-start.8
  91.0 2.2 copy-start.2
  91.0 43.5 %copy-start.6 = (f32[16,256]{1,0:T(8,128)S(1)}, f32[16,256]{1,0:T(8,128)}, u32[]{:S(2)}) copy-start(f32[16,256]{1,0:T(8,128)} %param.33) | copy-start | bytes 49156
  91.0 43.5 %copy-start.3 = (bf16[256,256]{1,0:T(8,128)(2,1)S(1)}, bf16[256,256]{1,0:T(8,128)(2,1)}, u32[]{:S(2)}) copy-start(bf16[256,256]{1,0:T(8,128)(2,1)} %param.31) | copy-start | bytes 393220
  91.0 43.5 %copy-start.9 = (f32[256]{0:T(256)S(1)}, f32[256]{0:T(256)}, u32[]{:S(2)}) copy-start(f32[256]{0:T(256)} %param.32) | copy-start | bytes 3076
  134.8 5.1 %copy-start.1 = (bf16[512,512]{1,0:T(8,128)(2,1)S(1)}, bf16[512,512]{1,0:T(8,128)(2,1)}, u32[]{:S(2)}) copy-start(bf16[512,512]{1,0:T(8,128)(2,1)} %param.40) | copy-start | bytes 1572868
  134.8 7.2 %copy-start.10 = (f32[256]{0:T(256)S(1)}, f32[256]{0:T(256)}, u32[]{:S(2)}) copy-start(f32[256]{0:T(256)} %param.34) | copy-start | bytes 3076
  142.0 139.1 %copy-start.5 = (bf16[24,128]{1,0:T(8,128)(2,1)S(1)}, bf16[24,128]{1,0:T(8,128)(2,1)}, u32[]{:S(2)}) copy-start(bf16[24,128]{1,0:T(8,128)(2,1)} %param.23) | copy-start | bytes 18436
Sparse Core Ops, SparseCore 0:
  146.5 134.5 reduce-scatter.1
